TPU v7x, 16 devices: a whole 2x2x2 slice. The times are simulated.
16 devices in a mesh: dp: 4 (over z, y), tp: 4 (over x, core).
Axes of the slice: x: 2, y: 2, z: 2, core: 2. Of those that a mesh axis runs over, the one named last changes fastest.
Arguments:
- x: bfloat16 [4, 128, 2560], P('dp', 'tp'), parts along dimension 0
- ln1_gamma: float32 [2560], replicated
- ln1_beta: float32 [2560], replicated
- w_qkv: bfloat16 [2560, 32, 3, 80], P(None, 'tp')
- b_qkv: float32 [32, 3, 80], P('tp')
- w_out: bfloat16 [2560, 2560], P('tp')
- b_out: float32 [2560], replicated
- ln2_gamma: float32 [2560], replicated
- ln2_beta: float32 [2560], replicated
- w_up: bfloat16 [2560, 10240], P(None, 'tp')
- b_up: float32 [10240], P('tp')
- w_down: bfloat16 [10240, 2560], P('tp')
- b_down: float32 [2560], replicated
- grad_y: bfloat16 [4, 128, 2560], P('dp', 'tp'), parts along dimension 0
Outputs:
- output 1: bfloat16 [4, 128, 2560], P('dp', 'tp'), parts along dimension 0
- output 2: bfloat16 [4, 128, 2560], P('dp', 'tp'), parts along dimension 0
- output 3: float32 [10240], P('dp'), parts along dimension 0
- output 4: float32 [10240], P('dp'), parts along dimension 0
- output 5: bfloat16 [10240, 32, 3, 80], P('dp', 'tp'), parts along dimension 0
- output 6: float32 [128, 3, 80], P(('dp', 'tp')), parts along dimension 0
- output 7: bfloat16 [10240, 2560], P(('dp', 'tp')), parts along dimension 0
- output 8: float32 [10240], P('dp'), parts along dimension 0
- output 9: float32 [10240], P('dp'), parts along dimension 0
- output 10: float32 [10240], P('dp'), parts along dimension 0
- output 11: bfloat16 [10240, 10240], P('dp', 'tp'), parts along dimension 0
- output 12: float32 [40960], P(('dp', 'tp')), parts along dimension 0
- output 13: bfloat16 [40960, 2560], P(('dp', 'tp')), parts along dimension 0
- output 14: float32 [10240], P('dp'), parts along dimension 0
There are 4 independent parts. A program takes and returns all parts, laid end to end along the dimension named above; an argument that names none is the same for every part.
All inputs are finite; a program needn't handle non-finite values.
Results may differ from a plain program's by a relative error of at most 0.0174444.
Values are sent between devices in bfloat16 or wider.
A program may use at most 1 GiB of HBM per device.

v0:
```python
import jax
import jax.numpy as jnp
from jax import lax
from jax.experimental import pallas as pl
from jax.experimental.pallas import tpu as pltpu
from jax.sharding import PartitionSpec as P

EPS = 1e-5
MASK_VALUE = -1e30
MESH = pl.DeviceIdType.MESH
F32 = jnp.float32
BF16 = jnp.bfloat16

D = 2560
SEQ = 128
TP = 4
ROWS = SEQ // TP
NH = 8
HD = 80
QKV = NH * 3 * HD
CTX = NH * HD
FF = 2560
AGC = 4
NS, NR = 24, 48
AGW = D // AGC
CHUNKS = (256, 256, 512, 512, 512, 256, 256)
Y_CHUNKS = (640,) * 4
OFF_G, OFF_ACT, OFF_QKV, OFF_O = 0, D, D + FF, D + FF + QKV
LROWS = D + FF + QKV + CTX
SLOPES = [2.0 ** (-(h + 1) / 4.0) for h in range(NH)]
NT = (((1,), (1,)), ((), ()))
NN = (((1,), (0,)), ((), ()))
TN = (((0,), (0,)), ((), ()))


def dot(a, b, dims):
    return lax.dot_general(a, b, dims, preferred_element_type=F32)


def ln_stats(v):
    mean = jnp.mean(v, axis=-1, keepdims=True)
    cen = v - mean
    var = jnp.mean(cen * cen, axis=-1, keepdims=True)
    rstd = lax.rsqrt(var + EPS)
    return cen * rstd, rstd


def ln_grad(dy, xhat, rstd, gain):
    dxh = dy * gain
    m1 = jnp.mean(dxh, axis=-1, keepdims=True)
    m2 = jnp.mean(dxh * xhat, axis=-1, keepdims=True)
    return rstd * (dxh - m1 - xhat * m2)


def block_kernel(x_hbm, gy_hbm, wq_hbm, wo_hbm, wu_hbm, wd_hbm, g1_hbm, b1_hbm, bq_hbm, bo_hbm, g2_hbm, b2_hbm, bu_hbm,
                 bd_hbm, y_hbm, gx_hbm, va_hbm, vb_hbm, gbu_hbm, l_hbm, r_hbm,
                 wq, wo, wu, wd, xh, g1, b1, bqv, bq, bo, g2, b2, bu, bd,
                 rbuf, lbuf, gbuf, qkvt, dqkv, ctx, dctxt, prob, act, dact, x1, xn1, xn2, rs, dmid, outb, gbu, va, vb,
                 pb, rx1, sb, rx2, wsem, lsem, osem, ssem, rsem):
    me = lax.axis_index('tp')
    ax = lax.div(me, 2)
    ak = lax.rem(me, 2)
    partner = 2 * ax + (1 - ak)
    cross = 2 * (1 - ax) + ak
    diag = 2 * (1 - ax) + (1 - ak)
    peers = (partner, cross, diag)

    def rows(i):
        return pl.ds(pl.multiple_of(i * ROWS, ROWS), ROWS)

    def block_rows(b):
        return rows(2 * b + ak)

    count = {'s': 0, 'r': 0}

    def alloc(kind, n=1):
        base = count[kind]
        count[kind] += n
        return base

    def remote(src, dst, si, ri, dev):
        return pltpu.make_async_remote_copy(src_ref=src, dst_ref=dst, send_sem=ssem.at[si], recv_sem=rsem.at[ri],
                                            device_id={'tp': dev}, device_id_type=MESH)

    x_load = pltpu.make_async_copy(x_hbm, xh.at[ax], lsem.at[0])
    x_load.start()
    small = [(g1_hbm, g1.at[0]), (b1_hbm, b1.at[0]), (bq_hbm, bqv), (bo_hbm, bo.at[0]), (g2_hbm, g2.at[0]), (b2_hbm, b2.at[0]),
             (bu_hbm, bu.at[0]), (bd_hbm, bd.at[0])]
    loads = [pltpu.make_async_copy(s, d, lsem.at[1 + i]) for i, (s, d) in enumerate(small)]
    for c in loads:
        c.start()
    gy_load = pltpu.make_async_copy(gy_hbm, rbuf.at[1, rows(me)], lsem.at[1 + len(small)])
    gy_load.start()
    wcopies = [pltpu.make_async_copy(s, d, wsem.at[i])
               for i, (s, d) in enumerate([(wq_hbm, wq), (wo_hbm, wo), (wd_hbm, wd), (wu_hbm, wu)])]

    bar = pltpu.get_barrier_semaphore()
    for dev in peers:
        pl.semaphore_signal(bar, inc=1, device_id={'tp': dev}, device_id_type=MESH)
    wcopies[0].start()
    wcopies[1].start()

    class Gather:
        def __init__(self, full):
            self.full = full
            self.s = alloc('s', 3)
            self.r = alloc('r', AGC + 2)

        def chunk(self, dev, c):
            return self.full.at[rows(dev), pl.ds(c * AGW, AGW)]

        def cross_copy(self, dev, c):
            ref = self.chunk(dev, c)
            return remote(ref, ref, self.s, self.r + c, cross)

        def fwd_copy(self, dev, c):
            ref = self.chunk(dev, c)
            return remote(ref, ref, self.s + 1, self.r + AGC, partner)

        def whole(self, dev, i, j, to):
            ref = self.full.at[rows(dev)]
            return remote(ref, ref, self.s + i, self.r + j, to)

        def own_copy(self, dev):
            return self.whole(dev, 2, AGC + 1, partner)

        def start(self):
            for c in range(AGC):
                self.cross_copy(me, c).start()
            self.own_copy(me).start()

        def forward(self, c):
            self.cross_copy(cross, c).wait_recv()
            self.fwd_copy(cross, c).start()

        def finish(self):
            self.own_copy(partner).wait_recv()
            self.whole(diag, 1, AGC, partner).wait_recv()

        def drain(self):
            self.whole(me, 0, 0, cross).wait_send()
            self.whole(cross, 1, AGC, partner).wait_send()
            self.own_copy(me).wait_send()

    class Share:
        def __init__(self, full):
            self.full = full
            self.s = alloc('s', 2)
            self.r = alloc('r', 2)

        def copy(self, b, k, i):
            ref = self.full.at[rows(2 * b + k)]
            return remote(ref, ref, self.s + i, self.r + i, partner)

        def send(self, b, i):
            self.copy(b, ak, i).start()

        def finish(self, b, i):
            self.copy(b, 1 - ak, i).wait_recv()

        def drain(self):
            self.copy(ax, ak, 0).wait_send()
            self.copy(1 - ax, ak, 1).wait_send()

    class Reduce:
        def __init__(self, i, both, chunks=CHUNKS):
            self.p, self.x1, self.sb, self.x2 = pb.at[i], rx1.at[i], sb.at[i], rx2.at[i]
            self.both = both
            self.chunks = chunks
            self.n = len(chunks)
            self.s = alloc('s', 2)
            self.r = alloc('r', self.n + 1)

        def cols(self, n):
            return pl.ds(sum(self.chunks[:n]), self.chunks[n])

        def pair(self, n):
            return remote(self.p.at[:, 1 - ak, :, self.cols(n)], self.x1.at[:, :, self.cols(n)], self.s, self.r + n, partner)

        def over(self, c):
            if self.both:
                src, dst = self.sb.at[:, :, c], self.x2.at[:, :, c]
            else:
                src, dst = self.sb.at[0, :, c], self.x2.at[0, :, c]
            return remote(src, dst, self.s + 1, self.r + self.n, cross)

        def produce(self, n, val):
            self.p[:, :, :, self.cols(n)] = val.astype(BF16).reshape(2, 2, ROWS, self.chunks[n])
            self.pair(n).start()

        def relay(self, n):
            self.pair(n).wait_recv()
            c = self.cols(n)
            if self.both:
                self.sb[:, :, c] = (self.p[:, ak, :, c].astype(F32) + self.x1[:, :, c].astype(F32)).astype(BF16)
            else:
                self.sb[0, :, c] = (self.p[1 - ax, ak, :, c].astype(F32) + self.x1[1 - ax, :, c].astype(F32)).astype(BF16)
            self.over(c).start()

        def run(self, fn, lag, also=None):
            for n in range(self.n):
                self.produce(n, fn(self.cols(n)))
                if n >= lag:
                    self.relay(n - lag)
                if also is not None:
                    also(n)

        def relay_from(self, first):
            for n in range(first, self.n):
                self.relay(n)

        def arrive(self):
            self.over(slice(None)).wait_recv()

        def block(self, b):
            return (self.sb[b].astype(F32) + self.x2[b].astype(F32)).astype(BF16).astype(F32)

        def own(self):
            v = self.p[ax, ak].astype(F32) + self.x1[ax].astype(F32) + self.x2[0].astype(F32)
            return v.astype(BF16).astype(F32)

        def drain(self):
            remote(self.p.at[:, 1 - ak], self.x1, self.s, self.r, partner).wait_send()
            self.over(slice(None)).wait_send()

    gat_m = Gather(rbuf.at[1])
    sh_h, sh_g, sh_a = Share(rbuf.at[2]), Share(gbuf), Share(rbuf.at[3])
    sc_a, sc_g, sc_y, sc_h = Reduce(0, True), Reduce(1, True), Reduce(2, False, Y_CHUNKS), Reduce(3, False)
    blocks = ((ax, 0), (1 - ax, 1))
    outs = []

    def emit(src, dst):
        c = pltpu.make_async_copy(src, dst, osem.at[len(outs)])
        c.start()
        outs.append(c)

    sx, rx = alloc('s'), alloc('r')
    x_load.wait()
    pl.semaphore_wait(bar, 3)
    remote(xh.at[ax], xh.at[ax], sx, rx, cross).start()
    for c in loads:
        c.wait()
    bq[...] = jnp.concatenate([bqv[t, h:h + 1, :] for h in range(NH) for t in range(3)], axis=1)
    for b, i in blocks:
        if i == 1:
            remote(xh.at[1 - ax], xh.at[1 - ax], sx, rx, cross).wait_recv()
        xhat, rstd = ln_stats(xh[b].astype(F32))
        if i == 0:
            xn1[...] = xhat
            rs[2] = jnp.broadcast_to(rstd, (ROWS, 128))
        rbuf[2, block_rows(b), :] = (xhat * g1[...] + b1[...]).astype(BF16)
        sh_h.send(b, i)
    gy_load.wait()
    gat_m.start()
    wcopies[2].start()
    wcopies[3].start()
    wcopies[0].wait()
    for b, i in blocks:
        sh_h.finish(b, i)
    emit(rbuf.at[2], r_hbm.at[2])

    QC = 640

    def qkv_body(n, carry):
        r0 = pl.multiple_of(n * QC, QC)
        v = dot(rbuf[2], wq[pl.ds(r0, QC), :], NT) + bq[:, pl.ds(r0, QC)]
        qkvt[pl.ds(r0, QC), :] = v.astype(BF16).T
        return carry
    lax.fori_loop(0, QKV // QC, qkv_body, 0)

    scale = HD ** -0.5
    jpos = lax.broadcasted_iota(jnp.int32, (SEQ, SEQ), 0)
    ipos = lax.broadcasted_iota(jnp.int32, (SEQ, SEQ), 1)
    causal = jpos <= ipos
    jf = jpos.astype(F32)
    base = jnp.where(me == 0, 1.0, jnp.where(me == 1, 0.25, jnp.where(me == 2, 0.0625, 0.015625))).astype(F32)

    def head(h, t):
        r0 = h * 3 * HD + t * HD
        return qkvt[r0:r0 + HD, :]

    for h in range(NH):
        s = dot(head(h, 1), head(h, 0), TN) * scale + (base * SLOPES[h]) * jf
        s = jnp.where(causal, s, MASK_VALUE)
        e = jnp.exp(s - jnp.max(s, axis=0, keepdims=True))
        p = e * (1.0 / jnp.sum(e, axis=0, keepdims=True))
        prob[h] = p
        lbuf[OFF_O + h * HD:OFF_O + (h + 1) * HD, :] = dot(head(h, 2), p.astype(BF16), NN).astype(BF16)
    for t in range(CTX // 128):
        ctx[:, t * 128:(t + 1) * 128] = lbuf[OFF_O + t * 128:OFF_O + (t + 1) * 128, :].T

    wcopies[1].wait()
    sc_a.run(lambda cols: dot(ctx[...], wo[:, cols], NN), 3)
    sc_a.relay_from(sc_a.n - 3)

    for c in range(AGC):
        gat_m.forward(c)
    wcopies[2].wait()
    gat_m.finish()
    emit(rbuf.at[1], r_hbm.at[1])
    FC = 512

    def dact_body(n, carry):
        f0 = pl.multiple_of(n * FC, FC)
        dact[:, pl.ds(f0, FC)] = dot(rbuf[1], wd[pl.ds(f0, FC), :], NT).astype(BF16)
        return carry
    lax.fori_loop(0, FF // FC, dact_body, 0)

    sc_a.arrive()
    for b, i in blocks:
        xm = xh[b].astype(F32) + sc_a.block(b) + bo[...]
        if i == 0:
            x1[...] = xm
        xhat, rstd = ln_stats(xm)
        xn2[b] = xhat
        rs[b] = jnp.broadcast_to(rstd, (ROWS, 128))
        gbuf[block_rows(b), :] = (xhat * g2[...] + b2[...]).astype(BF16)
        sh_g.send(b, i)
    wcopies[3].wait()
    for b, i in blocks:
        sh_g.finish(b, i)

    UC = 512
    k0 = 0.7978845608028654
    k1 = 0.044715

    for f0 in range(0, FF, UC):
        cols = pl.ds(f0, UC)
        v = dot(gbuf[...], wu[:, cols], NN) + bu[:, cols]
        v2 = v * v
        t = jnp.tanh(k0 * (v + k1 * (v2 * v)))
        hp = 0.5 * (1.0 + t)
        act[:, cols] = (v * hp).astype(BF16)
        dg = hp + (0.5 * k0) * v * (1.0 - t * t) * (1.0 + (3.0 * k1) * v2)
        dpre = dact[:, cols].astype(F32) * dg
        gbu[:, cols] = jnp.sum(dpre, axis=0, keepdims=True)
        rbuf[0, :, cols] = dpre.astype(BF16)
    emit(rbuf.at[0], r_hbm.at[0])
    emit(gbu, gbu_hbm)

    def dg_chunk(cols):
        return dot(rbuf[0], wu[cols, :], NT)
    sc_g.run(dg_chunk, 1)

    def rest(n):
        if n == 0:
            sc_g.relay(sc_g.n - 1)
    sc_y.run(lambda cols: dot(act[...], wd[:, cols], NN), sc_y.n, rest)
    va[3:4, :] = jnp.sum(rbuf[1, rows(me), :].astype(F32), axis=0, keepdims=True)

    sc_g.arrive()
    for b, i in blocks:
        dgl = sc_g.block(b)
        xhat, rstd = xn2[b], rs[b, :, 0:1]
        dm = rbuf[1, block_rows(b), :].astype(F32) + ln_grad(dgl, xhat, rstd, g2[...])
        rbuf[3, block_rows(b), :] = dm.astype(BF16)
        sh_a.send(b, i)
        if i == 0:
            dmid[...] = dm
    va[2:3, :] = jnp.sum(dmid[...], axis=0, keepdims=True)
    dgl = sc_g.block(ax)
    va[0:1, :] = jnp.sum(dgl * xn2[ax], axis=0, keepdims=True)
    va[1:2, :] = jnp.sum(dgl, axis=0, keepdims=True)

    sva, rva = alloc('s', 3), alloc('r', 3)

    def vec_copy(buf, hbm, s, r, i, owner, dev):
        return remote(buf, hbm.at[owner], s + i, r + i, dev)
    sc_y.relay_from(0)
    for i, dev in enumerate(peers):
        vec_copy(va, va_hbm, sva, rva, i, me, dev).start()
    emit(va, va_hbm.at[me])
    for b, i in blocks:
        sh_a.finish(b, i)
    emit(rbuf.at[3], r_hbm.at[3])

    ctx[...] = dot(rbuf[3], wo[...], NT).astype(BF16)
    for t in range(CTX // 128):
        dctxt[t * 128:(t + 1) * 128, :] = ctx[:, t * 128:(t + 1) * 128].T

    for h in range(NH):
        dot_h = dctxt[h * HD:(h + 1) * HD, :]
        p = prob[h]
        dp = dot(head(h, 2), dot_h, TN).astype(BF16).astype(F32)
        ds = (p * (dp - jnp.sum(dp * p, axis=0, keepdims=True))).astype(BF16)
        r0 = OFF_QKV + h * 3 * HD
        lbuf[r0:r0 + HD, :] = (dot(head(h, 1), ds, NN) * scale).astype(BF16)
        lbuf[r0 + HD:r0 + 2 * HD, :] = (dot(head(h, 0), ds, NT) * scale).astype(BF16)
        lbuf[r0 + 2 * HD:r0 + 3 * HD, :] = dot(dot_h, p.astype(BF16), NT).astype(BF16)
    for t in range(QKV // 128):
        dqkv[:, t * 128:(t + 1) * 128] = lbuf[OFF_QKV + t * 128:OFF_QKV + (t + 1) * 128, :].T
    emit(lbuf.at[pl.ds(OFF_QKV, QKV + CTX)], l_hbm.at[pl.ds(OFF_QKV, QKV + CTX)])

    sc_h.run(lambda cols: dot(dqkv[...], wq[:, cols], NN), 2)
    sc_h.relay_from(sc_h.n - 2)

    sc_y.arrive()
    outb[0] = (x1[...] + sc_y.own() + bd[...]).astype(BF16)
    emit(outb.at[0], y_hbm)
    def tr_body(src, off):
        def body(n, carry):
            r0 = pl.multiple_of(n * 512, 512)
            lbuf[pl.ds(off + r0, 512), :] = src[:, pl.ds(r0, 512)].T
            return carry
        return body
    lax.fori_loop(0, FF // 512, tr_body(act, OFF_ACT), 0)
    lax.fori_loop(0, D // 512, tr_body(gbuf, OFF_G), 0)
    emit(lbuf.at[pl.ds(0, OFF_QKV)], l_hbm.at[pl.ds(0, OFF_QKV)])

    sc_h.arrive()
    dhl = sc_h.own()
    xhat1, rstd1 = xn1[...], rs[2, :, 0:1]
    vb[0:1, :] = jnp.sum(dhl * xhat1, axis=0, keepdims=True)
    vb[1:2, :] = jnp.sum(dhl, axis=0, keepdims=True)
    svb, rvb = alloc('s', 3), alloc('r', 3)
    for i, dev in enumerate(peers):
        vec_copy(vb, vb_hbm, svb, rvb, i, me, dev).start()
    emit(vb, vb_hbm.at[me])
    outb[1] = (dmid[...] + ln_grad(dhl, xhat1, rstd1, g1[...])).astype(BF16)
    emit(outb.at[1], gx_hbm)
    remote(xh.at[ax], xh.at[ax], sx, rx, cross).wait_send()
    gat_m.drain()
    for g in (sh_h, sh_g, sh_a, sc_a, sc_g, sc_y, sc_h):
        g.drain()
    for i, dev in enumerate(peers):
        vec_copy(va, va_hbm, sva, rva, i, me, dev).wait_send()
        vec_copy(va, va_hbm, sva, rva, i, dev, dev).wait_recv()
    for i, dev in enumerate(peers):
        vec_copy(vb, vb_hbm, svb, rvb, i, dev, dev).wait_recv()
    for i, dev in enumerate(peers):
        vec_copy(vb, vb_hbm, svb, rvb, i, me, dev).wait_send()
    for c in outs:
        c.wait()
    assert (count['s'], count['r']) == (NS, NR), count


GR = 1280
SLOTS = 3
SECTIONS = ((OFF_ACT, FF, 1), (OFF_G, D, 0), (OFF_QKV, QKV, 2), (OFF_O, CTX, 3))
PIECES = (((160, 1), (160, 1), (320, 1), (640, 1), (GR, 1)), ((GR, 2),), ((GR, 1), (640, 1)), ((320, 1), (160, 1), (160, 1)))
SMALL = 8


def grad_kernel(y_in, gx_in, va_in, vb_in, gbu_in, l_hbm, r_hbm, y_out, gx_out, v0, v1, v2, v3, v4, v5, gbq_hbm, gbu_out,
                dwq, dwo, dwu, dwd, lv, rv, st, st2, yv, gxv, vav, vbv, vv, gv, gbq, isem, ssem, ssem2, psem, osem):
    loads = []
    for i, (off, n, r) in enumerate(SECTIONS):
        cl = pltpu.make_async_copy(l_hbm.at[pl.ds(off, n)], lv.at[pl.ds(off, n)], isem.at[2 * i])
        cr = pltpu.make_async_copy(r_hbm.at[r], rv.at[r], isem.at[2 * i + 1])
        cl.start()
        cr.start()
        loads.append((cl, cr))
    passes = [(y_in, yv, y_out), (gx_in, gxv, gx_out), (gbu_in, gv, gbu_out)]
    srcs = (yv, gxv, gv.at[0])
    pin = [pltpu.make_async_copy(a, b, psem.at[i]) for i, (a, b, _) in enumerate(passes)]
    pin.append(pltpu.make_async_copy(va_in, vav, psem.at[3]))
    pin.append(pltpu.make_async_copy(vb_in, vbv, psem.at[4]))
    for c in pin:
        c.start()
    douts = (dwd, dwu, dwq, dwo)
    step = 0

    def out_copy(slot, dst, r0):
        return pltpu.make_async_copy(st.at[slot], dst.at[pl.ds(r0, GR)], ssem.at[slot])
    smalls = []
    for i, (off, n, r) in enumerate(SECTIONS):
        loads[i][0].wait()
        loads[i][1].wait()
        dst = douts[i]
        r0 = 0
        for gr, times in PIECES[i]:
            if gr < GR:
                e = len(smalls)

                def small(m, carry, off=off + r0, gr=gr, e=e, r=r):
                    st2[e, 0:gr] = dot(lv[pl.ds(pl.multiple_of(off + m * gr, 32), gr), :], rv[r], NN).astype(BF16)
                    return carry
                lax.fori_loop(0, 1, small, 0)
                smalls.append(pltpu.make_async_copy(st2.at[e, pl.ds(0, gr)], dst.at[pl.ds(r0, gr)], ssem2.at[e]))
                smalls[-1].start()
            else:
                def body(m, carry, off=off + r0, r=r, dst=dst, step=step, r0=r0):
                    slot = lax.rem(m + step, SLOTS)

                    @pl.when(m + step >= SLOTS)
                    def _():
                        out_copy(slot, dwd, 0).wait()
                    st[slot] = dot(lv[pl.ds(pl.multiple_of(off + m * GR, 64), GR), :], rv[r], NN).astype(BF16)
                    out_copy(slot, dst, pl.multiple_of(r0 + m * GR, 64)).start()
                    return carry
                lax.fori_loop(0, times, body, 0)
                step += times
            r0 += gr * times
        if i == 0:
            for c in pin:
                c.wait()
            for buf, first, n in ((vav, 0, 4), (vbv, 4, 2)):
                tot = (buf[0] + buf[1]) + (buf[2] + buf[3])
                for j in range(n):
                    vv[first + j] = tot[j:j + 1]
        if i == 2:
            ones = jnp.ones((16, SEQ), BF16)
            for h in range(NH):
                for t in range(3):
                    q0 = OFF_QKV + h * 3 * HD + t * HD
                    gbq[t, h:h + 1, :] = dot(ones, lv[q0:q0 + HD, :], NT)[0:1]
    done = []
    for i, (_, _, o) in enumerate(passes):
        done.append(pltpu.make_async_copy(srcs[i], o, osem.at[i]))
    for i, o in enumerate((v0, v1, v2, v3, v4, v5)):
        done.append(pltpu.make_async_copy(vv.at[i, 0], o, osem.at[3 + i]))
    done.append(pltpu.make_async_copy(gbq, gbq_hbm, osem.at[9]))
    for c in done:
        c.start()
    for slot in range(SLOTS):
        out_copy(slot, dwd, 0).wait()
    for c in smalls:
        c.wait()
    for c in done:
        c.wait()


def solution(mesh):
    def local_step(x, ln1_gamma, ln1_beta, w_qkv, b_qkv, w_out, b_out, ln2_gamma, ln2_beta, w_up, b_up, w_down, b_down, grad_y):
        wqt = jnp.transpose(w_qkv, (1, 2, 3, 0)).reshape(QKV, D)
        any_spec = pl.BlockSpec(memory_space=pl.ANY)
        sds = jax.ShapeDtypeStruct
        y, gx, pva, pvb, gbu, lmat, rmat = pl.pallas_call(
            block_kernel,
            name='block',
            out_shape=(sds((ROWS, D), BF16), sds((ROWS, D), BF16), sds((TP, 4, D), F32), sds((TP, 2, D), F32), sds((1, FF), F32),
                       sds((LROWS, SEQ), BF16), sds((4, SEQ, D), BF16)),
            in_specs=[any_spec] * 14,
            out_specs=(any_spec,) * 7,
            scratch_shapes=[
                pltpu.VMEM((QKV, D), BF16), pltpu.VMEM((CTX, D), BF16), pltpu.VMEM((D, FF), BF16), pltpu.VMEM((FF, D), BF16),
                pltpu.VMEM((2, ROWS, D), BF16),
                pltpu.VMEM((1, D), F32), pltpu.VMEM((1, D), F32), pltpu.VMEM((3, NH, HD), F32), pltpu.VMEM((1, QKV), F32),
                pltpu.VMEM((1, D), F32), pltpu.VMEM((1, D), F32), pltpu.VMEM((1, D), F32), pltpu.VMEM((1, FF), F32), pltpu.VMEM((1, D), F32),
                pltpu.VMEM((4, SEQ, D), BF16), pltpu.VMEM((LROWS, SEQ), BF16), pltpu.VMEM((SEQ, D), BF16),
                pltpu.VMEM((QKV, SEQ), BF16), pltpu.VMEM((SEQ, QKV), BF16), pltpu.VMEM((SEQ, CTX), BF16),
                pltpu.VMEM((CTX, SEQ), BF16), pltpu.VMEM((NH, SEQ, SEQ), F32),
                pltpu.VMEM((SEQ, FF), BF16), pltpu.VMEM((SEQ, FF), BF16),
                pltpu.VMEM((ROWS, D), F32), pltpu.VMEM((ROWS, D), F32), pltpu.VMEM((2, ROWS, D), F32), pltpu.VMEM((3, ROWS, 128), F32),
                pltpu.VMEM((ROWS, D), F32), pltpu.VMEM((2, ROWS, D), BF16),
                pltpu.VMEM((1, FF), F32),
                pltpu.VMEM((4, D), F32), pltpu.VMEM((2, D), F32),
                pltpu.VMEM((4, 2, 2, ROWS, D), BF16), pltpu.VMEM((4, 2, ROWS, D), BF16),
                pltpu.VMEM((4, 2, ROWS, D), BF16), pltpu.VMEM((4, 2, ROWS, D), BF16),
                pltpu.SemaphoreType.DMA((4,)), pltpu.SemaphoreType.DMA((10,)), pltpu.SemaphoreType.DMA((11,)),
                pltpu.SemaphoreType.DMA((NS,)), pltpu.SemaphoreType.DMA((NR,)),
            ],
            compiler_params=pltpu.CompilerParams(collective_id=0, has_side_effects=True, vmem_limit_bytes=66_000_000),
            cost_estimate=pl.CostEstimate(flops=10_000_000_000, bytes_accessed=45_000_000, transcendentals=1_000_000),
        )(x[0], grad_y[0], wqt, w_out, w_up, w_down, ln1_gamma, ln1_beta, jnp.transpose(b_qkv, (1, 0, 2)), b_out,
          ln2_gamma, ln2_beta, b_up, b_down)
        y, gx, v0, v1, v2, v3, v4, v5, gbq, gbu, dwq, dwo, dwu, dwd = pl.pallas_call(
            grad_kernel,
            name='weight_grads',
            out_shape=(sds((ROWS, D), BF16), sds((ROWS, D), BF16)) + (sds((D,), F32),) * 6 + (
                sds((3, NH, HD), F32), sds((FF,), F32), sds((QKV, D), BF16), sds((CTX, D), BF16), sds((D, FF), BF16), sds((FF, D), BF16)),
            in_specs=[any_spec] * 7,
            out_specs=(any_spec,) * 14,
            scratch_shapes=[
                pltpu.VMEM((LROWS, SEQ), BF16), pltpu.VMEM((4, SEQ, D), BF16), pltpu.VMEM((SLOTS, GR, D), BF16), pltpu.VMEM((SMALL, 640, D), BF16),
                pltpu.VMEM((ROWS, D), BF16), pltpu.VMEM((ROWS, D), BF16), pltpu.VMEM((TP, 4, D), F32), pltpu.VMEM((TP, 2, D), F32),
                pltpu.VMEM((6, 1, D), F32), pltpu.VMEM((1, FF), F32),
                pltpu.VMEM((3, NH, HD), F32),
                pltpu.SemaphoreType.DMA((8,)), pltpu.SemaphoreType.DMA((SLOTS,)), pltpu.SemaphoreType.DMA((SMALL,)), pltpu.SemaphoreType.DMA((5,)), pltpu.SemaphoreType.DMA((10,)),
            ],
            compiler_params=pltpu.CompilerParams(vmem_limit_bytes=66_000_000),
            cost_estimate=pl.CostEstimate(flops=5_000_000_000, bytes_accessed=44_000_000, transcendentals=0),
        )(y, gx, pva, pvb, gbu, lmat, rmat)
        g_wqkv = jnp.transpose(dwq.reshape(NH, 3, HD, D), (3, 0, 1, 2))
        g_ln2g, g_ln2b, g_bo, g_bd, g_ln1g, g_ln1b = v0, v1, v2, v3, v4, v5
        return (y[None], gx[None], g_ln1g, g_ln1b, g_wqkv, jnp.transpose(gbq, (1, 0, 2)), dwo, g_bo,
                g_ln2g, g_ln2b, dwu, gbu, dwd, g_bd)

    row_spec = P('dp', 'tp', None)
    in_specs = (row_spec, P(), P(), P(None, 'tp', None, None), P('tp', None, None), P('tp', None), P(), P(), P(),
                P(None, 'tp'), P('tp'), P('tp', None), P(), row_spec)
    out_specs = (row_spec, row_spec, P('dp'), P('dp'), P('dp', 'tp', None, None), P(('dp', 'tp'), None, None),
                 P(('dp', 'tp'), None), P('dp'), P('dp'), P('dp'), P('dp', 'tp'), P(('dp', 'tp')), P(('dp', 'tp'), None), P('dp'))
    return jax.shard_map(local_step, mesh=mesh, in_specs=in_specs, out_specs=out_specs, check_vma=False)
```

profile of v0, /device:TPU:0, one launch (start us, length us, event | category | flops | bytes accessed | tf_op | source)
XLA Modules:
  0.0 72.6 jit_solution(2814099075845415760)
XLA Ops:
  0.7 55.7 %block.1 = (bf16[32,2560]{1,0:T(8,128)(2,1)}, bf16[32,2560]{1,0:T(8,128)(2,1)}, f32[4,4,2560]{2,1,0:T(4,128)}, f32[4,2,2560]{2,1,0:T(2,128)}, f32[1,2560]{1,0:T(...) custom-call(bf16[32,2560]{1,0:T(8,128)(2,1)} %bitcast.13, bf16[32,2560]{1,0:T(8,128)(2,1)} %bitcast.14, ...), custom_call_target="tpu_custom_call" | custom-call | flops 10000000000 | bytes 45000000 | tf_op jit(solution)/shard_map/block/pallas_call | solution.py:528
  56.4 16.0 %weight_grads.1 = (bf16[32,2560]{1,0:T(8,128)(2,1)}, bf16[32,2560]{1,0:T(8,128)(2,1)}, f32[2560]{0:T(1024)}, f32[2560]{0:T(1024)}, f32[2560]{0:T(1024)}, /*index...) custom-call(bf16[32,2560]{1,0:T(8,128)(2,1)} %get-tuple-element.35.y, ...), custom_call_target="tpu_custom_call" | custom-call | flops 5000000000 | bytes 44000000 | tf_op jit(solution)/shard_map/weight_grads/pallas_call | solution.py:557
where the time goes:
time: 72.7 us; the launch traced here: 72.6 us
  Pallas kernels  71.7 us (99%)
  between operations  0.84 us (1%)
    pallas_call x1, Pallas kernels, local_step(): pl.pallas_call(block_kernel, name='block', out_shape=(sds((ROWS, D), BF16...  55.7 us
    pallas_call x1, Pallas kernels, local_step(): pl.pallas_call(grad_kernel, name='weight_grads', out_shape=(sds((ROWS, D)...  16 us

commit v1 on v0

--- a/solution.py
+++ b/solution.py
@@ -434,11 +434,11 @@
     assert (count['s'], count['r']) == (NS, NR), count
 
 
-GR = 1280
-SLOTS = 3
+GR = 640
+SLOTS = 4
 SECTIONS = ((OFF_ACT, FF, 1), (OFF_G, D, 0), (OFF_QKV, QKV, 2), (OFF_O, CTX, 3))
-PIECES = (((160, 1), (160, 1), (320, 1), (640, 1), (GR, 1)), ((GR, 2),), ((GR, 1), (640, 1)), ((320, 1), (160, 1), (160, 1)))
-SMALL = 8
+PIECES = (((160, 1), (160, 1), (320, 1), (GR, 3)), ((GR, 4),), ((GR, 3),), ((320, 1), (160, 1), (160, 1)))
+SMALL = 6
 
 
 def grad_kernel(y_in, gx_in, va_in, vb_in, gbu_in, l_hbm, r_hbm, y_out, gx_out, v0, v1, v2, v3, v4, v5, gbq_hbm, gbu_out,
@@ -562,7 +562,7 @@
             in_specs=[any_spec] * 7,
             out_specs=(any_spec,) * 14,
             scratch_shapes=[
-                pltpu.VMEM((LROWS, SEQ), BF16), pltpu.VMEM((4, SEQ, D), BF16), pltpu.VMEM((SLOTS, GR, D), BF16), pltpu.VMEM((SMALL, 640, D), BF16),
+                pltpu.VMEM((LROWS, SEQ), BF16), pltpu.VMEM((4, SEQ, D), BF16), pltpu.VMEM((SLOTS, GR, D), BF16), pltpu.VMEM((SMALL, 320, D), BF16),
                 pltpu.VMEM((ROWS, D), BF16), pltpu.VMEM((ROWS, D), BF16), pltpu.VMEM((TP, 4, D), F32), pltpu.VMEM((TP, 2, D), F32),
                 pltpu.VMEM((6, 1, D), F32), pltpu.VMEM((1, FF), F32),
                 pltpu.VMEM((3, NH, HD), F32),

time: 72.7 us -> 72.1 us (level)
  no operation moved by 1% of the time
where the time goes in v1:
time: 72.1 us; the launch traced here: 72 us
  Pallas kernels  71.1 us (99%)
  between operations  0.84 us (1%)
    pallas_call x1, Pallas kernels, local_step(): pl.pallas_call(block_kernel, name='block', out_shape=(sds((ROWS, D), BF16...  55.7 us
    pallas_call x1, Pallas kernels, local_step(): pl.pallas_call(grad_kernel, name='weight_grads', out_shape=(sds((ROWS, D)...  15.4 us

profile of v1, /device:TPU:0, one launch (start us, length us, event | category | flops | bytes accessed | tf_op | source)
XLA Modules:
  0.0 72.0 jit_solution(17968645798438073330)
XLA Ops:
  0.7 55.7 %block.1 = (bf16[32,2560]{1,0:T(8,128)(2,1)}, bf16[32,2560]{1,0:T(8,128)(2,1)}, f32[4,4,2560]{2,1,0:T(4,128)}, f32[4,2,2560]{2,1,0:T(2,128)}, f32[1,2560]{1,0:T(...) custom-call(bf16[32,2560]{1,0:T(8,128)(2,1)} %bitcast.13, bf16[32,2560]{1,0:T(8,128)(2,1)} %bitcast.14, ...), custom_call_target="tpu_custom_call" | custom-call | flops 10000000000 | bytes 45000000 | tf_op jit(solution)/shard_map/block/pallas_call | solution.py:528
  56.4 15.4 %weight_grads.1 = (bf16[32,2560]{1,0:T(8,128)(2,1)}, bf16[32,2560]{1,0:T(8,128)(2,1)}, f32[2560]{0:T(1024)}, f32[2560]{0:T(1024)}, f32[2560]{0:T(1024)}, /*index...) custom-call(bf16[32,2560]{1,0:T(8,128)(2,1)} %get-tuple-element.35.y, ...), custom_call_target="tpu_custom_call" | custom-call | flops 5000000000 | bytes 44000000 | tf_op jit(solution)/shard_map/weight_grads/pallas_call | solution.py:557
